TPU v7x, 32 devices: a whole 2x2x4 slice. The times are simulated.
32 devices in a mesh: grp: 4 (over y, x), seq: 8 (over z, core).
Axes of the slice: x: 2, y: 2, z: 4, core: 2. Of those that a mesh axis runs over, the one named last changes fastest.
Arguments:
- queries: bfloat16 [8, 256, 8192], P('grp', 'seq'), parts along dimension 0, may hold values from -400 to 400
- stretch_keys: bfloat16 [8, 256, 1024], P('grp', 'seq'), parts along dimension 0, may hold values from -6 to 6
- stretch_values: bfloat16 [8, 256, 1024], P('grp', 'seq'), parts along dimension 0, may hold values from -6 to 6
- cache_keys: bfloat16 [8, 512, 1024], P('grp', 'seq'), parts along dimension 0, may hold values from -6 to 6
- cache_values: bfloat16 [8, 512, 1024], P('grp', 'seq'), parts along dimension 0, may hold values from -6 to 6
- prefix_len: int32 [8], P('grp'), parts along dimension 0, may hold values from 16 to 512, as said below
Outputs:
- attention: bfloat16 [8, 256, 8192], P('grp', 'seq'), parts along dimension 0
- prefix_bounds: bfloat16 [8, 32, 2048], P('grp', 'seq'), parts along dimension 0
- stretch_bounds: bfloat16 [8, 16, 2048], P('grp', 'seq'), parts along dimension 0
There are 4 independent parts, one for each index of `grp`. A program takes and returns all parts, laid end to end along the dimension named above; each array names one. Nothing has to cross between parts.
Inputs may be any that keep to these rules, and one draw needn't show every extreme that they name: `prefix_len`: multiples of 16; some sequence of every group has 512.
All inputs are finite; a program needn't handle non-finite values.
Results may differ from a plain program's by a relative error of at most 0.006.
Values may be sent and summed in bfloat16 or wider, within the bound.
A program may use at most 128 MiB of HBM per device.

v0:
```python
import math

import jax
import jax.numpy as jnp
from jax import lax
from jax.sharding import PartitionSpec as P

HQ = 64
HK = 8
DH = 128
PAGE = 16


def pick_block(length):
    for candidate in range(min(length, 512), 0, -1):
        if length % candidate == 0:
            return candidate
    return 1


def online(state, query_rows, query_pos, key_rows, value_rows, key_pos, from_cache, prefix_len):
    seqs, rows, _ = query_rows.shape
    group = HQ // HK
    factor = 1.0 / math.sqrt(DH)
    length = key_rows.shape[1]
    block = pick_block(length)
    steps_count = length // block
    shaped_query = query_rows.reshape(seqs, rows, HK, group, DH)
    key_blocks = jnp.moveaxis(key_rows.reshape(seqs, steps_count, block, HK, DH), 1, 0)
    value_blocks = jnp.moveaxis(value_rows.reshape(seqs, steps_count, block, HK, DH), 1, 0)
    pos_blocks = key_pos.reshape(steps_count, block)
    cache_blocks = from_cache.reshape(steps_count, block)
    top_length = jnp.max(prefix_len)
    top_query = jnp.max(query_pos)

    def one_step(current, pieces):
        key_part, value_part, pos_part, cache_part = pieces

        def compute(carried):
            running_top, running_sum, running_acc = carried
            scores = (
                jnp.einsum(
                    "srhgd,skhd->srhgk", shaped_query, key_part, preferred_element_type=jnp.float32
                )
                * factor
            )
            live = jnp.where(
                cache_part[None, None, :],
                pos_part[None, None, :] < prefix_len[:, None, None],
                pos_part[None, None, :] <= query_pos[None, :, None],
            )
            live = live[:, :, None, None, :]
            new_top = jnp.maximum(running_top, jnp.max(jnp.where(live, scores, -1e30), axis=-1))
            weights = jnp.where(live, jnp.exp(scores - new_top[..., None]), 0.0)
            shrink = jnp.exp(running_top - new_top)
            new_sum = running_sum * shrink + jnp.sum(weights, axis=-1)
            new_acc = running_acc * shrink[..., None] + jnp.einsum(
                "srhgk,skhd->srhgd",
                weights.astype(jnp.bfloat16),
                value_part,
                preferred_element_type=jnp.float32,
            )
            return (new_top, new_sum, new_acc)

        useful = jnp.any(jnp.where(cache_part, pos_part < top_length, pos_part <= top_query))
        return (lax.cond(useful, compute, lambda carried: carried, current), None)

    result, _ = lax.scan(one_step, state, (key_blocks, value_blocks, pos_blocks, cache_blocks))
    return result


def page_bounds(key_rows, live_pages):
    seqs, rows, width = key_rows.shape
    shaped = key_rows.reshape(seqs, rows // PAGE, PAGE, width)
    joined = jnp.concatenate([jnp.min(shaped, axis=2), jnp.max(shaped, axis=2)], axis=2)
    return jnp.where(live_pages[:, :, None], joined, jnp.zeros_like(joined))


def on_device(queries, stretch_keys, stretch_values, cache_keys, cache_values, prefix_len):
    seqs, ch_rows, _ = queries.shape
    pre_rows = cache_keys.shape[1]
    own_index = lax.axis_index("seq")
    group = HQ // HK
    groups = ((queries, own_index * ch_rows + jnp.arange(ch_rows, dtype=jnp.int32)),)
    states = tuple(
        (
            (
                jnp.full((seqs, entry[0].shape[1], HK, group), -1e30, jnp.float32),
                jnp.zeros((seqs, entry[0].shape[1], HK, group), jnp.float32),
                jnp.zeros((seqs, entry[0].shape[1], HK, group, DH), jnp.float32),
            )
            for entry in groups
        )
    )

    def absorb(current, key_rows, value_rows, key_pos, from_cache):
        return tuple(
            (
                online(
                    state, entry[0], entry[1], key_rows, value_rows, key_pos, from_cache, prefix_len
                )
                for state, entry in zip(current, groups)
            )
        )

    old_keys, old_values = (
        lax.all_gather(cache_keys, "seq", axis=1, tiled=True),
        lax.all_gather(cache_values, "seq", axis=1, tiled=True),
    )
    new_keys, new_values = (
        lax.all_gather(stretch_keys, "seq", axis=1, tiled=True),
        lax.all_gather(stretch_values, "seq", axis=1, tiled=True),
    )
    old_count = old_keys.shape[1]
    new_count = new_keys.shape[1]
    states = absorb(
        states,
        old_keys,
        old_values,
        jnp.arange(old_count, dtype=jnp.int32),
        jnp.ones((old_count,), bool),
    )
    states = absorb(
        states,
        new_keys,
        new_values,
        jnp.arange(new_count, dtype=jnp.int32),
        jnp.zeros((new_count,), bool),
    )
    outputs = [
        (state[2] / state[1][..., None])
        .reshape(seqs, state[2].shape[1], HQ * DH)
        .astype(jnp.bfloat16)
        for state in states
    ]
    attention = outputs[0]
    page_index = own_index * (pre_rows // PAGE) + jnp.arange(pre_rows // PAGE, dtype=jnp.int32)
    prefix_live = page_index[None, :] * PAGE < prefix_len[:, None]
    stretch_live = jnp.ones((seqs, ch_rows // PAGE), bool)
    return (
        attention,
        page_bounds(cache_keys, prefix_live),
        page_bounds(stretch_keys, stretch_live),
    )


def solution(mesh):
    return jax.shard_map(
        on_device,
        mesh=mesh,
        in_specs=(
            P("grp", "seq", None),
            P("grp", "seq", None),
            P("grp", "seq", None),
            P("grp", "seq", None),
            P("grp", "seq", None),
            P("grp"),
        ),
        out_specs=(P("grp", "seq", None), P("grp", "seq", None), P("grp", "seq", None)),
        check_vma=False,
    )
```

profile of v0, /device:TPU:0, one launch (start us, length us, event | category | flops | bytes accessed | tf_op | source)
XLA Modules:
  0.0 138.9 jit_solution(6246372038849168881)
XLA Ops:
  7.2 0.7 all-gather.5.cloned.1.call-update
  8.0 0.7 all-gather.7.cloned.1.call-update
  8.7 0.7 all-gather.11.cloned.1.call-update
  10.0 1.5 %copy.52 = bf16[8,8,64,128]{3,2,1,0:T(8,128)(2,1)S(1)} copy(bf16[8,8,64,128]{3,1,2,0:T(8,128)(2,1)} %bitcast.84) | data formatting | bytes 2097152
  12.2 1.3 fusion.28
  14.7 1.3 compare_reduce_fusion
  16.9 0.6 broadcast_in_dim.141
  17.5 1.0 bitcast_reduce_fusion.3
  19.4 0.7 maximum_select_fusion
  20.1 21.4 %all-gather.5.cloned.1.call-done = bf16[2,512,1024]{2,1,0:T(8,128)(2,1)} async-done(((bf16[2,64,1024]{2,1,0:T(8,128)(2,1)}), bf16[2,512,1024]{2,1,0:T(8,128)(2,1)}) %all-gather.5.cloned.1.call-update) | async-done | bytes 2097168 | tf_op jit(solution)/shard_map/all_gather | solution.py:107
  41.5 30.2 %all-gather.7.cloned.1.call-done = bf16[2,512,1024]{2,1,0:T(8,128)(2,1)} async-done(((bf16[2,64,1024]{2,1,0:T(8,128)(2,1)}), bf16[2,512,1024]{2,1,0:T(8,128)(2,1)}) %all-gather.7.cloned.1.call-update) | async-done | bytes 2097168 | tf_op jit(solution)/shard_map/all_gather | solution.py:108
  71.7 19.0 %conditional.2 = ((f32[2,32,8,8]{1,3,2,0:T(8,128)S(1)}, f32[2,32,8,8]{1,3,2,0:T(8,128)}, f32[2,32,8,8,128]{4,3,1,2,0:T(8,128)S(1)})) conditional(s32[]{:T(128)} %convert_element_type.24, (f32[2,32,8,8]{1,3,2,0:T(8,128)S(1)}, f32[2,32,8,8]{1,3,2,0:T(8,128)}, f32[2,32,8,8,128]{4,3,1,2,0:T(8,128)S(1)}) %tuple.36, (s32[512]{0:T(512)S(1)}, ...), branch_computations={%region_4.5_spmd, %region_5.8_spmd} | conditional | flops 1091576832 | bytes 68441152 | solution.py:66
  71.8 2.2 %copy.48 = bf16[128,8,8,128]{3,2,1,0:T(8,128)(2,1)S(1)} copy(bf16[128,8,8,128]{3,1,2,0:T(8,128)(2,1)} %bitcast.82) | data formatting | bytes 4194304 | tf_op jit(solution)/shard_map/while/body/eval_jaxpr/cond
  74.1 2.5 %fusion = (f32[2,32,8,8]{1,3,2,0:T(8,128)S(1)}, f32[2,8,512,32,8]{2,3,4,1,0:T(8,128)S(1)}) fusion(pred[2,512]{1,0:T(4,128)(4,1)S(1)} %broadcast_compare_fusion, bf16[2,32,8,8,128]{4,3,2,1,0:T(8,128)(2,1)S(1)} %get-tuple-element.213, bf16[2,512,8,128,1]{3,2,1,0,4:T(8,128)(2,1)S(1)} %bitcast_bitcast_fusion.1), kind=kOutput, calls=%fused_computation.2 | convolution fusion | flops 543158272 | bytes 11551744 | tf_op jit(solution)/shard_map/while/body/eval_jaxpr/cond/branch_1_fun/srhgd,skhd->srhgk/dot_general | solution.py:42
  76.6 3.6 %fusion.3 = (bf16[2,32,8,8,512]{4,1,3,2,0:T(8,128)(2,1)}, f32[2,32,8,8]{1,3,2,0:T(8,128)S(1)}) fusion(f32[2,8,512,32,8]{2,3,4,1,0:T(8,128)S(1)} %get-tuple-element.255, f32[2,32,8,8]{1,3,2,0:T(8,128)S(1)} %max.7, pred[2,512]{1,0:T(4,128)(4,1)S(1)} %broadcast_compare_fusion), kind=kLoop, calls=%fused_computation.5 | loop fusion | flops 10481664 | bytes 12616704 | tf_op jit(solution)/shard_map/while/body/eval_jaxpr/cond/branch_1_fun/convert_element_type | solution.py:59
  80.2 1.5 %multiply_add_fusion = (f32[2,32,8,8]{1,3,2,0:T(8,128)}, f32[2,32,8,8]{1,3,2,0:T(8,128)}) fusion(f32[2,32,8,8]{1,3,2,0:T(8,128)S(1)} %get-tuple-element.253, f32[2,32,8,8]{1,3,2,0:T(8,128)} %get-tuple-element.184, f32[2,32,8,8]{1,3,2,0:T(8,128)S(1)} %get-tuple-element.179, f32[2,32,8,8]{1,3,2,0:T(8,128)S(1)} %max.7), kind=kLoop, calls=%fused_computation.16 | loop fusion | flops 12288 | bytes 98304 | tf_op jit(solution)/shard_map/while/body/eval_jaxpr/cond/branch_1_fun/add | solution.py:56
  81.7 1.0 copy.20
  82.7 2.2 %copy.49 = bf16[128,8,8,128]{3,2,1,0:T(8,128)(2,1)S(1)} copy(bf16[128,8,8,128]{3,1,2,0:T(8,128)(2,1)} %bitcast.83) | data formatting | bytes 4194304 | tf_op jit(solution)/shard_map/while/body/eval_jaxpr/cond
  85.1 2.1 %copy-done.1 = bf16[2,32,8,8,512]{4,1,3,2,0:T(8,128)(2,1)S(1)} copy-done((bf16[2,32,8,8,512]{4,1,3,2,0:T(8,128)(2,1)S(1)}, bf16[2,32,8,8,512]{4,1,3,2,0:T(8,128)(2,1)}, u32[]{:S(2)}) %copy-start.1) | copy-done | bytes 4194328 | tf_op jit(solution)/shard_map/while/body/eval_jaxpr/cond
  87.2 3.4 %bitcast_add_fusion = f32[2,32,8,8,128]{4,3,1,2,0:T(8,128)S(1)} fusion(f32[2,32,8,8,128]{4,3,1,2,0:T(8,128)S(1)} %get-tuple-element.185, bf16[2,512,8,128,1]{3,2,1,0,4:T(8,128)(2,1)S(1)} %bitcast_bitcast_fusion, bf16[2,32,8,8,512]{4,1,3,2,0:T(8,128)(2,1)S(1)} %copy-done.1, f32[2,32,8,8]{3,1,2,0:T(8,128)S(1)} %copy.20), kind=kOutput, calls=%fused_computation.11 | convolution fusion | flops 537919488 | bytes 10502144 | tf_op jit(solution)/shard_map/while/body/eval_jaxpr/cond/branch_1_fun/srhgk,skhd->srhgd/dot_general | solution.py:57
  90.7 4.3 %all-gather.11.cloned.1.call-done = bf16[2,256,1024]{2,1,0:T(8,128)(2,1)} async-done(((bf16[2,32,1024]{2,1,0:T(8,128)(2,1)}), bf16[2,256,1024]{2,1,0:T(8,128)(2,1)}) %all-gather.11.cloned.1.call-update) | async-done | bytes 1048592 | tf_op jit(solution)/shard_map/all_gather | solution.py:112
  95.0 23.3 %all-gather.9.cloned.1.call-done = bf16[2,256,1024]{2,1,0:T(8,128)(2,1)} async-done(((bf16[2,32,1024]{2,1,0:T(8,128)(2,1)}), bf16[2,256,1024]{2,1,0:T(8,128)(2,1)}) %all-gather.9.cloned.1.call-update) | async-done | bytes 1048592 | tf_op jit(solution)/shard_map/all_gather | solution.py:111
  118.3 10.8 %conditional.3 = ((f32[2,32,8,8]{1,3,2,0:T(8,128)}, f32[2,32,8,8,128]{4,3,1,2,0:T(8,128)S(1)})) conditional(s32[]{:T(128)} %convert_element_type.23, (f32[2,32,8,8]{1,3,2,0:T(8,128)}, f32[2,32,8,8,128]{4,3,1,2,0:T(8,128)S(1)}) %tuple.38, (s32[256]{0:T(256)S(1)}, s32[32]{0:T(128)S(1)}, bf16[2,256,1024]{2,1,0:T(8,128)(2,1)}, ...), branch_computations={%region_8.9_spmd, %region_9.12_spmd.clone} | conditional | flops 546324480 | bytes 41166032 | solution.py:66
  118.4 1.5 %copy.50 = bf16[64,8,8,128]{3,2,1,0:T(8,128)(2,1)S(1)} copy(bf16[64,8,8,128]{3,1,2,0:T(8,128)(2,1)} %bitcast.86) | data formatting | bytes 2097152 | tf_op jit(solution)/shard_map/while/body/eval_jaxpr/cond
  119.9 1.4 fusion.15
  121.3 2.5 %fusion.18 = (bf16[2,32,8,8,256]{4,1,3,2,0:T(8,128)(2,1)}, f32[2,32,8,8]{1,3,2,0:T(8,128)S(1)}) fusion(f32[2,8,256,32,8]{2,3,4,1,0:T(8,128)S(1)} %get-tuple-element.259, f32[2,32,8,8]{1,3,2,0:T(8,128)S(1)} %max.9, pred[32,256]{1,0:T(8,128)(4,1)S(1)} %broadcast_compare_fusion.1), kind=kLoop, calls=%fused_computation.24 | loop fusion | flops 5238784 | bytes 6332416 | tf_op jit(solution)/shard_map/while/body/eval_jaxpr/cond/branch_1_fun/convert_element_type | solution.py:59
  123.8 1.5 %multiply_add_fusion.1 = (f32[2,32,8,8]{1,3,2,0:T(8,128)}, f32[2,32,8,8]{1,3,2,0:T(8,128)S(1)}) fusion(f32[2,32,8,8]{1,3,2,0:T(8,128)S(1)} %get-tuple-element.257, f32[2,32,8,8]{1,3,2,0:T(8,128)} %get-tuple-element.233, f32[2,32,8,8]{1,3,2,0:T(8,128)S(1)} %get-tuple-element.232, f32[2,32,8,8]{1,3,2,0:T(8,128)S(1)} %max.9), kind=kLoop, calls=%fused_computation.35 | loop fusion | flops 12288 | bytes 98304 | tf_op jit(solution)/shard_map/while/body/eval_jaxpr/cond/branch_1_fun/add | solution.py:56
  125.8 1.2 copy-done
  127.0 2.0 %bitcast_add_fusion.1 = f32[2,32,8,8,128]{4,3,1,2,0:T(8,128)S(1)} fusion(f32[2,32,8,8,128]{4,3,1,2,0:T(8,128)S(1)} %get-tuple-element.234, bf16[2,32,8,8,256]{4,1,3,2,0:T(8,128)(2,1)S(1)} %copy-done, bf16[2,256,8,128,1]{3,2,1,0,4:T(8,128)(2,1)S(1)} %bitcast_bitcast_fusion.2, f32[2,32,8,8]{3,1,2,0:T(8,128)S(1)} %copy.43), kind=kOutput, calls=%fused_computation.26 | convolution fusion | flops 269484032 | bytes 7356416 | tf_op jit(solution)/shard_map/while/body/eval_jaxpr/cond/branch_1_fun/srhgk,skhd->srhgd/dot_general | solution.py:57
  129.1 1.0 copy.29
  130.1 0.7 divide_convert_fusion
  131.1 1.3 convert_element_type.26
  (36 shorter events, 4.3 us)
Async XLA Ops:
  7.2 4.4 %copy-start.4 = (s32[2]{0:T(128)S(1)}, s32[2]{0:T(128)}, u32[]{:S(2)}) copy-start(s32[2]{0:T(128)} %param.15) | copy-start | bytes 28
  7.2 34.3 %all-gather.5.cloned.1.call-start = ((), (), s32[]{:S(2)}) async-start(), calls=%async_computation | async-start | bytes 2359296 | tf_op jit(solution)/shard_map/all_gather | solution.py:107
  7.9 63.8 %all-gather.7.cloned.1.call-start = ((), (), s32[]{:S(2)}) async-start(), calls=%async_computation.1 | async-start | bytes 2359296 | tf_op jit(solution)/shard_map/all_gather | solution.py:108
  8.7 86.3 %all-gather.11.cloned.1.call-start = ((), (), s32[]{:S(2)}) async-start(), calls=%async_computation.3 | async-start | bytes 1179648 | tf_op jit(solution)/shard_map/all_gather | solution.py:112
  9.4 108.9 %all-gather.9.cloned.1.call-start = ((), (), s32[]{:S(2)}) async-start(), calls=%async_computation.2 | async-start | bytes 1179648 | tf_op jit(solution)/shard_map/all_gather | solution.py:111
  10.0 8.6 %copy-start.3 = (bf16[2,64,1024]{2,1,0:T(8,128)(2,1)S(1)}, bf16[2,64,1024]{2,1,0:T(8,128)(2,1)}, u32[]{:S(2)}) copy-start(bf16[2,64,1024]{2,1,0:T(8,128)(2,1)} %param.13) | copy-start | bytes 786436
  84.9 2.3 %copy-start.1 = (bf16[2,32,8,8,512]{4,1,3,2,0:T(8,128)(2,1)S(1)}, bf16[2,32,8,8,512]{4,1,3,2,0:T(8,128)(2,1)}, u32[]{:S(2)}) copy-start(bf16[2,32,8,8,512]{4,1,3,2,0:T(8,128)(2,1)} %get-tuple-element.252) | copy-start | bytes 12582916 | tf_op jit(solution)/shard_map/while/body/eval_jaxpr/cond
  121.3 4.1 %copy-start.2 = (bf16[2,256,1024]{2,1,0:T(8,128)(2,1)S(1)}, bf16[2,256,1024]{2,1,0:T(8,128)(2,1)}, u32[]{:S(2)}) copy-start(bf16[2,256,1024]{2,1,0:T(8,128)(2,1)} %get-tuple-element.235) | copy-start | bytes 3145732 | tf_op jit(solution)/shard_map/while/body/eval_jaxpr/cond
  125.4 1.6 %copy-start = (bf16[2,32,8,8,256]{4,1,3,2,0:T(8,128)(2,1)S(1)}, bf16[2,32,8,8,256]{4,1,3,2,0:T(8,128)(2,1)}, u32[]{:S(2)}) copy-start(bf16[2,32,8,8,256]{4,1,3,2,0:T(8,128)(2,1)} %get-tuple-element.256) | copy-start | bytes 6291460 | tf_op jit(solution)/shard_map/while/body/eval_jaxpr/cond
Sparse Core Ops, SparseCore 0:
  9.6 31.8 all-gather.4
  43.1 28.5 all-gather.6
  73.3 21.6 all-gather.10
  96.4 21.8 all-gather.8
where the time goes:
time: 139 us
  waiting for transfers between devices  81.8 us (59%)
  other arithmetic  16.4 us (12%)
  local copies, waits for them, and re-layouts  15.9 us (11%)
  between operations  15.2 us (11%)
  matrix products  9.3 us (7%)
    all_gather x1, waiting for transfers between devices, on_device(): lax.all_gather(cache_values, 'seq', axis=1, tiled=True)  30.2 us
    all_gather x1, waiting for transfers between devices, on_device(): lax.all_gather(stretch_keys, 'seq', axis=1, tiled=True)  23.3 us
    all_gather x1, waiting for transfers between devices, on_device(): lax.all_gather(cache_keys, 'seq', axis=1, tiled=True)  21.4 us
    cond x11, local copies, waits for them, and re-layouts  9.53 us
    convert_element_type x2, other arithmetic, compute(): weights.astype(jnp.bfloat16)  6.11 us
    dot_general x2, matrix products, compute(): jnp.einsum('srhgk,skhd->srhgd', weights.astype(jnp.bfloat16), value_part,...  5.48 us
    all_gather x1, waiting for transfers between devices, on_device(): lax.all_gather(stretch_values, 'seq', axis=1, tiled=True)  4.29 us
    dot_general x2, matrix products, compute(): jnp.einsum('srhgd,skhd->srhgk', shaped_query, key_part, preferred_element...  3.81 us
  transfers between devices with their start and end apart: 4, of which 4 were waited for; matrix products, arithmetic and copies ran while one was open for 18% of the time, Pallas kernels for 0%

commit v1 on v0

v1 whole, which is shorter than its diff:
```python
import functools
import math

import jax
import jax.numpy as jnp
from jax import lax
from jax.experimental import pallas as pl
from jax.experimental.pallas import tpu as pltpu
from jax.sharding import PartitionSpec as P

HQ = 64
HK = 8
DH = 128
PAGE = 16
GROUP = HQ // HK
HALF = HK // 2
WIDE = GROUP * DH
SHIP = 2
MESH = pl.DeviceIdType.MESH
MASKED = -1e30


def kernel(n, q, sk, sv, ck, cv, plen, out, pb, sb, kv, qall, oall, bias, ckv, skv, qsem, lsem, dsend, drecv,
           qmsend, qmrecv, rsend, rrecv, lsend, lrecv, xsend, xrecv, ssend, srecv, oloc, osend, orecv, posend, porecv, bsem):
    seqs, rows, _ = q.shape
    pre = ck.shape[1]
    chips = n // 2
    last = chips - 1
    cache_keys = n * pre
    me = lax.axis_index("seq")
    c, k = me // 2, me % 2
    mate = c * 2 + (1 - k)
    reach = jnp.maximum(c, last - c)

    def remote(src, dst, send, recv, target):
        return pltpu.make_async_remote_copy(
            src_ref=src, dst_ref=dst, send_sem=send, recv_sem=recv, device_id={"seq": target}, device_id_type=MESH)

    sources = ((ck, 0, 0, pre), (cv, 1, 0, pre), (sk, 0, cache_keys, rows), (sv, 1, cache_keys, rows))

    def own_copy(h, i):
        src, which, base, length = sources[i]
        lanes = pl.ds(pl.multiple_of((k * HALF + h) * DH, DH), DH)
        return pltpu.make_async_copy(
            src.at[:, :, lanes], kv.at[h, which, :, pl.ds(base + me * length, length), :], lsem.at[h, i])

    def mate_copy(h, i):
        src, which, base, length = sources[i]
        lanes = pl.ds(pl.multiple_of(((1 - k) * HALF + h) * DH, DH), DH)
        return remote(src.at[:, :, lanes], kv.at[h, which, :, pl.ds(base + me * length, length), :],
                      dsend.at[h, i], drecv.at[h, i], mate)

    def wide_lanes(core, h):
        return pl.ds(pl.multiple_of((core * HALF + h) * WIDE, WIDE), WIDE)

    def own_q(h):
        return pltpu.make_async_copy(q.at[:, :, wide_lanes(k, h)], qall.at[0, h, :, k], qsem.at[h])

    def mate_q(h):
        return remote(q.at[:, :, wide_lanes(1 - k, h)], qall.at[0, h, :, k], qmsend.at[h], qmrecv.at[h], mate)

    def ship_q(h, core, target):
        return remote(q.at[:, :, wide_lanes(core, h)], qall.at[1, h, :, k], xsend.at[h, core], xrecv.at[h, k], target)

    def cache_rows(j):
        return pl.ds(pl.multiple_of(j * 2 * pre, 2 * pre), 2 * pre)

    def stretch_rows(j):
        return pl.ds(pl.multiple_of(cache_keys + j * 2 * rows, 2 * rows), 2 * rows)

    def right_copy(h, j, part):
        where = kv.at[h, :, :, cache_rows(j) if part == 0 else stretch_rows(j), :]
        return remote(where, where, rsend.at[h, j, part], rrecv.at[h, j, part], jnp.minimum(me + 2, n - 1))

    def left_copy(h, j):
        where = kv.at[h, :, :, cache_rows(j), :]
        return remote(where, where, lsend.at[h, j], lrecv.at[h, j], jnp.maximum(me - 2, 0))

    def ship_stretch(h):
        where = kv.at[h, :, :, stretch_rows(last), :]
        return remote(where, where, ssend.at[h], srecv.at[h], jnp.maximum(me - 2, 0))

    def out_own(h):
        return pltpu.make_async_copy(oall.at[0, h, :, k], out.at[:, :, wide_lanes(k, h)], oloc.at[h])

    def out_mate(h):
        return remote(oall.at[0, h, :, 1 - k], out.at[:, :, wide_lanes(k, h)], osend.at[h], orecv.at[h], mate)

    def out_ship(h, dev):
        return remote(oall.at[1, h, :, dev], out.at[:, :, wide_lanes(k, h)], posend.at[h, dev], porecv.at[h, k],
                      last * 2 + dev)

    for h in range(HALF):
        for i in range(4):
            own_copy(h, i).start()
    bound_copies = (pltpu.make_async_copy(ck, ckv, bsem.at[0]), pltpu.make_async_copy(sk, skv, bsem.at[1]))
    for copy in bound_copies:
        copy.start()
    for h in range(HALF):
        own_q(h).start()

    @pl.loop(c + 1, chips)
    def _(j):
        for h in range(HALF):
            kv[h, :, :, stretch_rows(j), :] = jnp.zeros((2, seqs, 2 * rows, DH), jnp.bfloat16)

    barrier = pltpu.get_barrier_semaphore()
    pl.semaphore_signal(barrier, inc=1, device_id={"seq": mate}, device_id_type=MESH)

    @pl.when(c > 0)
    def _():
        for core in range(2):
            pl.semaphore_signal(barrier, inc=1, device_id={"seq": (c - 1) * 2 + core}, device_id_type=MESH)

    @pl.when(c < last)
    def _():
        for core in range(2):
            pl.semaphore_signal(barrier, inc=1, device_id={"seq": (c + 1) * 2 + core}, device_id_type=MESH)

    pl.semaphore_wait(barrier, 1 + 2 * (c > 0).astype(jnp.int32) + 2 * (c < last).astype(jnp.int32))

    for h in range(HALF):
        for i in range(4):
            mate_copy(h, i).start()
    for h in range(HALF):
        @pl.when((c < last) | (h >= SHIP))
        def _():
            mate_q(h).start()

    def bounds_of(keys, s, live):
        pages = keys.shape[1] // PAGE
        block = keys[s].astype(jnp.float32).reshape(pages, PAGE, HK * DH)
        low, high = jnp.min(block, axis=1), jnp.max(block, axis=1)
        if live is not None:
            low, high = jnp.where(live, low, 0.0), jnp.where(live, high, 0.0)
        return low.astype(jnp.bfloat16), high.astype(jnp.bfloat16)

    def local_work():
        token = lax.broadcasted_iota(jnp.int32, (rows, n * rows), 0)
        col = lax.broadcasted_iota(jnp.int32, (rows, n * rows), 1)
        slot = lax.broadcasted_iota(jnp.int32, (rows, cache_keys), 1)
        for s in range(seqs):
            cached = jnp.where(slot < plen[s], 0.0, MASKED)
            for side in range(2):
                first = (c if side == 0 else last) * 2 * rows
                for dev in range(2):
                    bias[side, s, dev, :, :cache_keys] = cached
                    bias[side, s, dev, :, cache_keys:] = jnp.where(col <= token + (first + dev * rows), 0.0, MASKED)
        for copy in bound_copies:
            copy.wait()
        width = HK * DH
        for s in range(seqs):
            page = me * (pre // PAGE) + lax.broadcasted_iota(jnp.int32, (pre // PAGE, width), 0)
            low, high = bounds_of(ckv, s, page * PAGE < plen[s])
            pb[s, :, :width] = low
            pb[s, :, width:] = high
            low, high = bounds_of(skv, s, None)
            sb[s, :, :width] = low
            sb[s, :, width:] = high

    def attend(h, side, s, dev):
        scale = math.log2(math.e) / math.sqrt(DH)
        query = jnp.concatenate([qall[side, h, s, dev, :, g * DH:(g + 1) * DH] for g in range(GROUP)], axis=0)
        scores = lax.dot_general(query, kv[h, 0, s], (((1,), (1,)), ((), ())), preferred_element_type=jnp.float32)
        keys = scores.shape[1]
        scores = scores.reshape(GROUP, rows, keys) + bias[side, s, dev][None]
        scores = scores.reshape(GROUP * rows, keys)
        top = jnp.max(scores, axis=1, keepdims=True)
        weights = jnp.exp2((scores - top) * scale)
        total = jnp.sum(weights, axis=1, keepdims=True)
        mixed = jnp.dot(weights.astype(jnp.bfloat16), kv[h, 1, s], preferred_element_type=jnp.float32)
        mixed = (mixed / total).astype(jnp.bfloat16)
        for g in range(GROUP):
            oall[side, h, s, dev, :, g * DH:(g + 1) * DH] = mixed[g * rows:(g + 1) * rows]

    def shipped(h):
        return h < SHIP

    def from_left(h, d):
        return (c - d >= 0) & jnp.logical_not((c == last) & shipped(h))

    def to_right(h, d):
        return (c < last) & (c - d >= 0) & jnp.logical_not((c + 1 == last) & shipped(h))

    def to_left(h, d):
        return (c > 0) & (c + d <= last)

    def one_slot(t):
        @pl.loop(0, HALF)
        def _(back):
            h = HALF - 1 - back
            d = t - h

            @pl.when((d >= 0) & (d <= last))
            def _():
                @pl.when(d == 0)
                def _():
                    for i in range(4):
                        own_copy(h, i).wait()
                        mate_copy(h, i).wait_recv()

                @pl.when((d > 0) & from_left(h, d))
                def _():
                    for part in range(2):
                        right_copy(h, c - d, part).wait_recv()

                @pl.when(to_right(h, d))
                def _():
                    for part in range(2):
                        right_copy(h, c - d, part).start()

                @pl.when((d > 0) & (c + d <= last))
                def _():
                    left_copy(h, c + d).wait_recv()

                @pl.when(to_left(h, d))
                def _():
                    left_copy(h, c + d).start()

                @pl.when((d == 0) & (c == last) & shipped(h))
                def _():
                    for core in range(2):
                        ship_q(h, core, (last - 1) * 2 + core).start()
                    ship_stretch(h).start()

        h = t - reach
        @pl.when((h >= 0) & (h < HALF) & ((c < last) | jnp.logical_not(shipped(h))))
        def _():
            extra = (c == last - 1) & shipped(h)

            @pl.when(extra)
            def _():
                for core in range(2):
                    remote(q.at[:, :, wide_lanes(core, h)], qall.at[1, h, :, core], xsend.at[h, core],
                           xrecv.at[h, core], mate).wait_recv()
                ship_stretch(h).wait_recv()

            own_q(h).wait()
            remote(q.at[:, :, wide_lanes(k, h)], qall.at[0, h, :, 1 - k], qmsend.at[h], qmrecv.at[h], mate).wait_recv()

            @pl.loop(jnp.where(extra, 0, 2 * seqs), 4 * seqs)
            def _(step):
                mine = step // (2 * seqs)
                rest = step % (2 * seqs)
                attend(h, 1 - mine, rest // 2, rest % 2)

                @pl.when(step == 2 * seqs - 1)
                def _():
                    for dev in range(2):
                        out_ship(h, dev).start()

            out_own(h).start()
            out_mate(h).start()

    one_slot(0)
    local_work()

    @pl.loop(1, HALF + last)
    def _(t):
        one_slot(t)

    @pl.loop(0, HALF)
    def _(h):
        for i in range(4):
            mate_copy(h, i).wait_send()

        @pl.when((c < last) | jnp.logical_not(shipped(h)))
        def _():
            mate_q(h).wait_send()
            out_own(h).wait()
            out_mate(h).wait_send()
            remote(oall.at[0, h, :, k], out.at[:, :, wide_lanes(1 - k, h)], osend.at[h], orecv.at[h], mate).wait_recv()

        @pl.when((c == last) & shipped(h))
        def _():
            own_q(h).wait()
            ship_stretch(h).wait_send()
            for core in range(2):
                ship_q(h, core, (last - 1) * 2 + core).wait_send()
                remote(oall.at[0, h, :, k], out.at[:, :, wide_lanes(core, h)], posend.at[h, core], porecv.at[h, core],
                       mate).wait_recv()

        @pl.when((c == last - 1) & shipped(h))
        def _():
            for dev in range(2):
                out_ship(h, dev).wait_send()

        @pl.loop(0, chips)
        def _(d):
            @pl.when(to_right(h, d))
            def _():
                for part in range(2):
                    right_copy(h, c - d, part).wait_send()

            @pl.when(to_left(h, d))
            def _():
                left_copy(h, c + d).wait_send()


def on_device(n, queries, stretch_keys, stretch_values, cache_keys, cache_values, prefix_len):
    seqs, rows, width = queries.shape
    pre = cache_keys.shape[1]
    chips = n // 2
    keys = n * (pre + rows)
    dma = pltpu.SemaphoreType.DMA
    hbm = pl.BlockSpec(memory_space=pl.ANY)
    vmem = pl.BlockSpec(memory_space=pltpu.VMEM)
    return pl.pallas_call(
        functools.partial(kernel, n),
        out_shape=(
            jax.ShapeDtypeStruct((seqs, rows, width), jnp.bfloat16),
            jax.ShapeDtypeStruct((seqs, pre // PAGE, 2 * HK * DH), jnp.bfloat16),
            jax.ShapeDtypeStruct((seqs, rows // PAGE, 2 * HK * DH), jnp.bfloat16),
        ),
        in_specs=[hbm] * 5 + [pl.BlockSpec(memory_space=pltpu.SMEM)],
        out_specs=(hbm, vmem, vmem),
        scratch_shapes=[
            pltpu.VMEM((HALF, 2, seqs, keys, DH), jnp.bfloat16),
            pltpu.VMEM((2, HALF, seqs, 2, rows, WIDE), jnp.bfloat16),
            pltpu.VMEM((2, HALF, seqs, 2, rows, WIDE), jnp.bfloat16),
            pltpu.VMEM((2, seqs, 2, rows, keys), jnp.float32),
            pltpu.VMEM((seqs, pre, HK * DH), jnp.bfloat16),
            pltpu.VMEM((seqs, rows, HK * DH), jnp.bfloat16),
            dma((HALF,)),
            dma((HALF, 4)),
            dma((HALF, 4)), dma((HALF, 4)),
            dma((HALF,)), dma((HALF,)),
            dma((HALF, chips, 2)), dma((HALF, chips, 2)),
            dma((HALF, chips)), dma((HALF, chips)),
            dma((HALF, 2)), dma((HALF, 2)),
            dma((HALF,)), dma((HALF,)),
            dma((HALF,)),
            dma((HALF,)), dma((HALF,)),
            dma((HALF, 2)), dma((HALF, 2)),
            dma((2,)),
        ],
        compiler_params=pltpu.CompilerParams(
            collective_id=0, has_side_effects=True, vmem_limit_bytes=60 * 1024 * 1024),
    )(queries, stretch_keys, stretch_values, cache_keys, cache_values, prefix_len)


def solution(mesh):
    rows = P("grp", "seq", None)
    return jax.shard_map(
        functools.partial(on_device, mesh.shape["seq"]),
        mesh=mesh,
        in_specs=(rows, rows, rows, rows, rows, P("grp")),
        out_specs=(rows, rows, rows),
        check_vma=False,
    )
```

time: 139 us -> 65.2 us (0.47)
  the two profiles are of different devices: /device:TPU:0 before, /device:TPU:27 now
where the time goes in v1:
time: 65.2 us; the launch traced here: 65 us
  Pallas kernels  60.7 us (93%)
  local copies, waits for them, and re-layouts  3.61 us (6%)
    pallas_call x1, Pallas kernels, on_device(): pl.pallas_call(functools.partial(kernel, n), out_shape=(jax.ShapeDtypeStr...  60.7 us
    unnamed x7, local copies, waits for them, and re-layouts  3.61 us

profile of v1, /device:TPU:27, one launch (start us, length us, event | category | flops | bytes accessed | tf_op | source)
XLA Modules:
  0.0 65.0 jit_solution(10962573784714155619)
XLA Ops:
  0.6 60.7 %shard_map.85 = (bf16[2,32,8192]{2,1,0:T(8,128)(2,1)}, bf16[2,4,2048]{2,1,0:T(4,128)(2,1)}, bf16[2,2,2048]{2,1,0:T(2,128)(2,1)}) custom-call(bf16[2,32,8192]{2,1,0:T(8,128)(2,1)} %q.1, bf16[2,32,1024]{2,1,0:T(8,128)(2,1)} %sk.1, bf16[2,32,1024]{2,1,0:T(8,128)(2,1)} %sv.1, bf16[2,64,1024]{2,1,0:T(8,128)(2,1)} %ck.1, bf16[2,64,1024]{2,1,0:T(8,128)(2,1)} %cv.1, ...), custom_call_target="tpu_custom_call" | custom-call | tf_op jit(solution)/shard_map/pallas_call | solution.py:308
  61.3 0.0 copy-start
  61.4 2.3 %copy.12 = bf16[2,32,8192]{2,1,0:T(8,128)(2,1)} copy(bf16[2,32,8192]{2,1,0:T(8,128)(2,1)} %get-tuple-element.6) | data formatting | bytes 2097152
  63.6 0.0 copy-done
  63.6 0.0 copy-start.1
  63.6 0.6 copy.13
  64.2 0.1 copy-done.1
  64.4 0.6 copy.14
Async XLA Ops:
  61.3 2.3 %copy-start = (bf16[2,4,2048]{2,1,0:T(4,128)(2,1)S(1)}, bf16[2,4,2048]{2,1,0:T(4,128)(2,1)}, u32[]{:S(2)}) copy-start(bf16[2,4,2048]{2,1,0:T(4,128)(2,1)} %get-tuple-element.7) | copy-start | bytes 98308
  63.6 0.7 %copy-start.1 = (bf16[2,2,2048]{2,1,0:T(2,128)(2,1)S(1)}, bf16[2,2,2048]{2,1,0:T(2,128)(2,1)}, u32[]{:S(2)}) copy-start(bf16[2,2,2048]{2,1,0:T(2,128)(2,1)} %get-tuple-element.8) | copy-start | bytes 49156

commit v2 on v1

v2 whole, which is shorter than its diff:
```python
import functools
import math

import jax
import jax.numpy as jnp
from jax import lax
from jax.experimental import pallas as pl
from jax.experimental.pallas import tpu as pltpu
from jax.sharding import PartitionSpec as P

HQ = 64
HK = 8
DH = 128
PAGE = 16
GROUP = HQ // HK
HALF = HK // 2
WIDE = GROUP * DH
SHIP = 5
LEAD = 1
MESH = pl.DeviceIdType.MESH
MASKED = -1e30


def kernel(n, q, sk, sv, ck, cv, plen, out, pb, sb, kv, qall, oall, bias, ckv, skv, qsem, lsem, dsend, drecv,
           qmsend, qmrecv, rsend, rrecv, lsend, lrecv, xsend, xrecv, ssend, srecv, oloc, osend, orecv, posend, porecv, bsem):
    seqs, rows, _ = q.shape
    pre = ck.shape[1]
    chips = n // 2
    last = chips - 1
    cache_keys = n * pre
    me = lax.axis_index("seq")
    c, k = me // 2, me % 2
    mate = c * 2 + (1 - k)
    units = HALF * seqs
    reach = jnp.maximum(c, last - c)

    def remote(src, dst, send, recv, target):
        return pltpu.make_async_remote_copy(
            src_ref=src, dst_ref=dst, send_sem=send, recv_sem=recv, device_id={"seq": target}, device_id_type=MESH)

    sources = ((ck, 0, 0, pre), (cv, 1, 0, pre), (sk, 0, cache_keys, rows), (sv, 1, cache_keys, rows))

    def place(ref, side, u, dev):
        return ref.at[side, u // seqs, u % seqs, dev]

    def keys_of(u, which, span):
        return kv.at[u // seqs, which, u % seqs, span, :]

    def both_of(u, span):
        return kv.at[u // seqs, :, u % seqs, span, :]

    def lanes_of(core, u):
        return pl.ds(pl.multiple_of((core * HALF + u // seqs) * DH, DH), DH)

    def own_copy(u, i):
        src, which, base, length = sources[i]
        return pltpu.make_async_copy(
            src.at[u % seqs, :, lanes_of(k, u)], keys_of(u, which, pl.ds(base + me * length, length)), lsem.at[u, i])

    def mate_copy(u, i):
        src, which, base, length = sources[i]
        return remote(src.at[u % seqs, :, lanes_of(1 - k, u)], keys_of(u, which, pl.ds(base + me * length, length)),
                      dsend.at[u, i], drecv.at[u, i], mate)

    def wide(ref, core, u):
        return ref.at[u % seqs, :, pl.ds(pl.multiple_of((core * HALF + u // seqs) * WIDE, WIDE), WIDE)]

    def own_q(u):
        return pltpu.make_async_copy(wide(q, k, u), place(qall, 0, u, k), qsem.at[u])

    def mate_q(u, dev):
        return remote(wide(q, 1 - k, u), place(qall, 0, u, dev), qmsend.at[u], qmrecv.at[u], mate)

    def ship_q(u, core, dev):
        return remote(wide(q, core, u), place(qall, 1, u, dev), xsend.at[u, core], xrecv.at[u, dev],
                      jnp.maximum(last - 1, 0) * 2 + core)

    def cache_rows(j):
        return pl.ds(pl.multiple_of(j * 2 * pre, 2 * pre), 2 * pre)

    def stretch_rows(j):
        return pl.ds(pl.multiple_of(cache_keys + j * 2 * rows, 2 * rows), 2 * rows)

    def right_copy(u, j, part):
        where = both_of(u, cache_rows(j) if part == 0 else stretch_rows(j))
        return remote(where, where, rsend.at[u, j, part], rrecv.at[u, j, part], jnp.minimum(me + 2, n - 1))

    def left_copy(u, j):
        where = both_of(u, cache_rows(j))
        return remote(where, where, lsend.at[u, j], lrecv.at[u, j], jnp.maximum(me - 2, 0))

    def ship_stretch(u):
        where = both_of(u, stretch_rows(last))
        return remote(where, where, ssend.at[u], srecv.at[u], jnp.maximum(me - 2, 0))

    def out_own(u):
        return pltpu.make_async_copy(place(oall, 0, u, k), wide(out, k, u), oloc.at[u])

    def out_mate(u, core):
        return remote(place(oall, 0, u, 1 - k), wide(out, core, u), osend.at[u], orecv.at[u], mate)

    def out_ship(u, dev, core):
        return remote(place(oall, 1, u, dev), wide(out, core, u), posend.at[u, dev], porecv.at[u, core],
                      last * 2 + dev)

    for u in range(units):
        for i in range(4):
            own_copy(u, i).start()
    bound_copies = (pltpu.make_async_copy(ck, ckv, bsem.at[0]), pltpu.make_async_copy(sk, skv, bsem.at[1]))
    for u in range(units):
        own_q(u).start()
    for copy in bound_copies:
        copy.start()

    @pl.loop(c + 1, chips)
    def _(j):
        for h in range(HALF):
            kv[h, :, :, stretch_rows(j), :] = jnp.zeros((2, seqs, 2 * rows, DH), jnp.bfloat16)

    barrier = pltpu.get_barrier_semaphore()
    pl.semaphore_signal(barrier, inc=1, device_id={"seq": mate}, device_id_type=MESH)

    @pl.when(c > 0)
    def _():
        for core in range(2):
            pl.semaphore_signal(barrier, inc=1, device_id={"seq": (c - 1) * 2 + core}, device_id_type=MESH)

    @pl.when(c < last)
    def _():
        for core in range(2):
            pl.semaphore_signal(barrier, inc=1, device_id={"seq": (c + 1) * 2 + core}, device_id_type=MESH)

    pl.semaphore_wait(barrier, 1 + 2 * (c > 0).astype(jnp.int32) + 2 * (c < last).astype(jnp.int32))

    for u in range(units):
        for i in range(4):
            mate_copy(u, i).start()
    for u in range(units):
        @pl.when((c < last) | (u < units - SHIP))
        def _():
            mate_q(u, k).start()

    def bounds_of(keys, s, live):
        pages = keys.shape[1] // PAGE
        block = keys[s].astype(jnp.float32).reshape(pages, PAGE, HK * DH)
        low, high = jnp.min(block, axis=1), jnp.max(block, axis=1)
        if live is not None:
            low, high = jnp.where(live, low, 0.0), jnp.where(live, high, 0.0)
        return low.astype(jnp.bfloat16), high.astype(jnp.bfloat16)

    def local_work():
        token = lax.broadcasted_iota(jnp.int32, (rows, n * rows), 0)
        col = lax.broadcasted_iota(jnp.int32, (rows, n * rows), 1)
        slot = lax.broadcasted_iota(jnp.int32, (rows, cache_keys), 1)
        for s in range(seqs):
            cached = jnp.where(slot < plen[s], 0.0, MASKED)
            for side in range(2):
                first = (c if side == 0 else last) * 2 * rows
                for dev in range(2):
                    bias[side, s, dev, :, :cache_keys] = cached
                    bias[side, s, dev, :, cache_keys:] = jnp.where(col <= token + (first + dev * rows), 0.0, MASKED)
        for copy in bound_copies:
            copy.wait()
        width = HK * DH
        for s in range(seqs):
            page = me * (pre // PAGE) + lax.broadcasted_iota(jnp.int32, (pre // PAGE, width), 0)
            low, high = bounds_of(ckv, s, page * PAGE < plen[s])
            pb[s, :, :width] = low
            pb[s, :, width:] = high
            low, high = bounds_of(skv, s, None)
            sb[s, :, :width] = low
            sb[s, :, width:] = high

    def attend(u, side):
        scale = math.log2(math.e) / math.sqrt(DH)
        h, s = u // seqs, u % seqs
        for dev in range(2):
            query = jnp.concatenate([qall[side, h, s, dev, :, g * DH:(g + 1) * DH] for g in range(GROUP)], axis=0)
            scores = lax.dot_general(query, kv[h, 0, s], (((1,), (1,)), ((), ())), preferred_element_type=jnp.float32)
            keys = scores.shape[1]
            scores = scores.reshape(GROUP, rows, keys) + bias[side, s, dev][None]
            scores = scores.reshape(GROUP * rows, keys)
            top = jnp.max(scores, axis=1, keepdims=True)
            weights = jnp.exp2((scores - top) * scale)
            total = jnp.sum(weights, axis=1, keepdims=True)
            mixed = jnp.dot(weights.astype(jnp.bfloat16), kv[h, 1, s], preferred_element_type=jnp.float32)
            mixed = (mixed / total).astype(jnp.bfloat16)
            for g in range(GROUP):
                oall[side, h, s, dev, :, g * DH:(g + 1) * DH] = mixed[g * rows:(g + 1) * rows]

    def shipped(u):
        return u >= units - SHIP

    def from_left(u, d):
        return (c - d >= 0) & jnp.logical_not((c == last) & shipped(u))

    def to_right(u, d):
        return (c < last) & (c - d >= 0) & jnp.logical_not((c + 1 == last) & shipped(u))

    def to_left(u, d):
        return (c > 0) & (c + d <= last)

    def own_ready(u):
        @pl.when(u < units)
        def _():
            for i in range(4):
                own_copy(u, i).wait()
                mate_copy(u, i).wait_recv()

            @pl.when(c < last)
            def _():
                @pl.when(to_right(u, 0))
                def _():
                    for part in range(2):
                        right_copy(u, c, part).start()

            @pl.when(c > 0)
            def _():
                left_copy(u, c).start()

            @pl.when((c == last) & shipped(u))
            def _():
                ship_stretch(u).start()

        given = u + min(LEAD, units - SHIP)

        @pl.when((c == last) & (given < units) & shipped(given))
        def _():
            for core in range(2):
                ship_q(given, core, k).start()

    def one_slot(t):
        own_ready(t)

        @pl.loop(1, chips)
        def _(d):
            u = t - d

            @pl.when((u >= 0) & (u < units))
            def _():
                @pl.when(from_left(u, d))
                def _():
                    for part in range(2):
                        right_copy(u, c - d, part).wait_recv()

                @pl.when(to_right(u, d))
                def _():
                    for part in range(2):
                        right_copy(u, c - d, part).start()

        @pl.loop(1, chips)
        def _(d):
            u = t - d

            @pl.when((u >= 0) & (u < units) & (c + d <= last))
            def _():
                left_copy(u, c + d).wait_recv()

                @pl.when(to_left(u, d))
                def _():
                    left_copy(u, c + d).start()

        u = t - reach

        @pl.when((u >= 0) & (u < units) & ((c < last) | jnp.logical_not(shipped(u))))
        def _():
            extra = (c == last - 1) & shipped(u)

            @pl.when(extra)
            def _():
                for dev in range(2):
                    ship_q(u, k, dev).wait_recv()
                ship_stretch(u).wait_recv()

            own_q(u).wait()
            mate_q(u, 1 - k).wait_recv()

            @pl.loop(jnp.where(extra, 0, 1), 2)
            def _(step):
                attend(u, 1 - step)

                @pl.when(step == 0)
                def _():
                    for dev in range(2):
                        out_ship(u, dev, k).start()

            out_own(u).start()
            out_mate(u, k).start()

    one_slot(0)
    local_work()

    @pl.loop(1, units + last)
    def _(t):
        one_slot(t)

    @pl.loop(0, units)
    def _(u):
        for i in range(4):
            mate_copy(u, i).wait_send()

        @pl.when((c < last) | jnp.logical_not(shipped(u)))
        def _():
            mate_q(u, k).wait_send()
            out_own(u).wait()
            out_mate(u, k).wait_send()
            out_mate(u, 1 - k).wait_recv()

        @pl.when((c == last) & shipped(u))
        def _():
            own_q(u).wait()
            ship_stretch(u).wait_send()
            for core in range(2):
                ship_q(u, core, k).wait_send()
                out_ship(u, k, core).wait_recv()

        @pl.when((c == last - 1) & shipped(u))
        def _():
            for dev in range(2):
                out_ship(u, dev, k).wait_send()

        @pl.loop(0, chips)
        def _(d):
            @pl.when(to_right(u, d))
            def _():
                for part in range(2):
                    right_copy(u, c - d, part).wait_send()

            @pl.when(to_left(u, d))
            def _():
                left_copy(u, c + d).wait_send()


def on_device(n, queries, stretch_keys, stretch_values, cache_keys, cache_values, prefix_len):
    seqs, rows, width = queries.shape
    pre = cache_keys.shape[1]
    chips = n // 2
    units = HALF * seqs
    keys = n * (pre + rows)
    dma = pltpu.SemaphoreType.DMA
    hbm = pl.BlockSpec(memory_space=pl.ANY)
    vmem = pl.BlockSpec(memory_space=pltpu.VMEM)
    return pl.pallas_call(
        functools.partial(kernel, n),
        out_shape=(
            pltpu.VMEM((seqs, rows, width), jnp.bfloat16),
            pltpu.VMEM((seqs, pre // PAGE, 2 * HK * DH), jnp.bfloat16),
            pltpu.VMEM((seqs, rows // PAGE, 2 * HK * DH), jnp.bfloat16),
        ),
        in_specs=[hbm] * 5 + [pl.BlockSpec(memory_space=pltpu.SMEM)],
        out_specs=(vmem, vmem, vmem),
        scratch_shapes=[
            pltpu.VMEM((HALF, 2, seqs, keys, DH), jnp.bfloat16),
            pltpu.VMEM((2, HALF, seqs, 2, rows, WIDE), jnp.bfloat16),
            pltpu.VMEM((2, HALF, seqs, 2, rows, WIDE), jnp.bfloat16),
            pltpu.VMEM((2, seqs, 2, rows, keys), jnp.float32),
            pltpu.VMEM((seqs, pre, HK * DH), jnp.bfloat16),
            pltpu.VMEM((seqs, rows, HK * DH), jnp.bfloat16),
            dma((units,)),
            dma((units, 4)),
            dma((units, 4)), dma((units, 4)),
            dma((units,)), dma((units,)),
            dma((units, chips, 2)), dma((units, chips, 2)),
            dma((units, chips)), dma((units, chips)),
            dma((units, 2)), dma((units, 2)),
            dma((units,)), dma((units,)),
            dma((units,)),
            dma((units,)), dma((units,)),
            dma((units, 2)), dma((units, 2)),
            dma((2,)),
        ],
        compiler_params=pltpu.CompilerParams(
            collective_id=0, has_side_effects=True, vmem_limit_bytes=60 * 1024 * 1024),
    )(queries, stretch_keys, stretch_values, cache_keys, cache_values, prefix_len)


def solution(mesh):
    rows = P("grp", "seq", None)
    return jax.shard_map(
        functools.partial(on_device, mesh.shape["seq"]),
        mesh=mesh,
        in_specs=(rows, rows, rows, rows, rows, P("grp")),
        out_specs=(rows, rows, rows),
        check_vma=False,
    )
```

time: 65.2 us -> 55.4 us (0.85)
  the two profiles are of different devices: /device:TPU:27 before, /device:TPU:0 now
where the time goes in v2:
time: 55.4 us; the launch traced here: 55.3 us
  Pallas kernels  52.4 us (95%)
  local copies, waits for them, and re-layouts  2.19 us (4%)
  between operations  0.64 us (1%)
    pallas_call x1, Pallas kernels, on_device(): pl.pallas_call(functools.partial(kernel, n), out_shape=(pltpu.VMEM((seqs,...  52.4 us
    unnamed x3, local copies, waits for them, and re-layouts  2.19 us

profile of v2, /device:TPU:0, one launch (start us, length us, event | category | flops | bytes accessed | tf_op | source)
XLA Modules:
  0.0 55.3 jit_solution(16036936909738621081)
XLA Ops:
  0.6 52.4 %shard_map.85 = (bf16[2,32,8192]{2,1,0:T(8,128)(2,1)S(1)}, bf16[2,4,2048]{2,1,0:T(4,128)(2,1)S(1)}, bf16[2,2,2048]{2,1,0:T(2,128)(2,1)S(1)}) custom-call(bf16[2,32,8192]{2,1,0:T(8,128)(2,1)} %q.1, bf16[2,32,1024]{2,1,0:T(8,128)(2,1)} %sk.1, bf16[2,32,1024]{2,1,0:T(8,128)(2,1)} %sv.1, bf16[2,64,1024]{2,1,0:T(8,128)(2,1)} %ck.1, bf16[2,64,1024]{2,1,0:T(8,128)(2,1)} %cv.1, ...), custom_call_target="tpu_custom_call" | custom-call | tf_op jit(solution)/shard_map/pallas_call | solution.py:343
  53.1 1.0 %copy.12 = bf16[2,32,8192]{2,1,0:T(8,128)(2,1)} copy(bf16[2,32,8192]{2,1,0:T(8,128)(2,1)S(1)} %get-tuple-element.3) | data formatting | bytes 2097152
  54.0 0.6 %copy.14 = bf16[2,2,2048]{2,1,0:T(2,128)(2,1)} copy(bf16[2,2,2048]{2,1,0:T(2,128)(2,1)S(1)} %get-tuple-element.5) | data formatting | bytes 32768
  54.6 0.6 %copy.13 = bf16[2,4,2048]{2,1,0:T(4,128)(2,1)} copy(bf16[2,4,2048]{2,1,0:T(4,128)(2,1)S(1)} %get-tuple-element.4) | data formatting | bytes 65536
